TPU v7x, 32 devices: a whole 2x2x4 slice. The times are simulated.
32 devices in a mesh: gx: 4 (over y, core), gy: 8 (over z, x).
Axes of the slice: x: 2, y: 2, z: 4, core: 2. Of those that a mesh axis runs over, the one named last changes fastest.
Arguments:
- thermal_anomaly: float32 [32, 128, 1024], P(None, 'gx', 'gy'), may hold values from -6 to 6
- ambient_diffusion: bfloat16 [128, 1024], P('gx', 'gy'), may hold values from 0.019897461 to 0.25
- solar_light: bfloat16 [128, 1024], P('gx', 'gy'), may hold values from 0.5 to 4
- sea_tile_flags: int32 [4, 8, 64], P('gx', 'gy'), may hold values 0 or 1
- flooded_layer_tally: int32 [4, 8, 64], P('gx', 'gy'), may hold values from 1 to 32
- tile_holder_rank: int32 [4, 8, 64, 1], P('gx', 'gy'), may hold values from 0 to 7; in each aligned block of 64 rows (0 to 63, 64 to 127, ..., all dimensions but the last counted through in order) at most 16 rows name the same one
- solute_amounts: float32 [4, 8, 128, 8, 2048], P('gx', 'gy'), may hold values from 0.09 to 11
- reaction_rates: float32 [8, 8], replicated, may hold values from -0.2 to 0.5
Outputs:
- thermal_final: float32 [32, 128, 1024], P(None, 'gx', 'gy')
- solute_final: float32 [4, 8, 128, 8, 2048], P('gx', 'gy')
Inputs may be any that keep to these rules, and one draw needn't show every extreme that they name: `tile_holder_rank`: among the 64 blocks of one device, at most 16 name the same owner, a bound that some block reaches of them.
All inputs are finite; a program needn't handle non-finite values. No bound on the sum of `sea_tile_flags` on one device may be relied on, other than what follows from the above.
Results may differ from a plain program's by a relative error of at most 0.0003.
Values may be sent and summed in bfloat16 or wider, within the bound.
No kernel may reach another device: no remote copies, remote signals or barrier semaphores. Data moves between devices by JAX's collectives and lax.ppermute only.
A program may use at most 128 MiB of HBM per device.

v0:
```python
import jax
import jax.numpy as jnp
from jax import lax
from jax.sharding import PartitionSpec as P

NU_COEF = 0.2
STEP_DT = 0.05
ATTEN_WATER = 0.06
ATTEN_CHL = 0.05
WARMING_SCALE = 0.5
GROWTH_TEMP = 0.063


def with_halo(cells, sides, width):
    for axis, dim in sides:
        count = lax.axis_size(axis)
        ends = count - 1
        head = lax.slice_in_dim(cells, 0, width, axis=dim)
        tail = lax.slice_in_dim(cells, cells.shape[dim] - width, cells.shape[dim], axis=dim)
        cells = jnp.concatenate(
            [
                lax.ppermute(tail, axis, [(i, (i + 1) % count) for i in range(ends)]),
                cells,
                lax.ppermute(head, axis, [((i + 1) % count, i) for i in range(ends)]),
            ],
            axis=dim,
        )
    return cells


def masked_step(field, within_layer):
    center = field[:, 1:-1, 1:-1]
    span_east = center.shape[1]
    span_north = center.shape[2]
    total = jnp.zeros_like(center)
    for first, second in ((0, 1), (2, 1), (1, 0), (1, 2)):
        near = field[:, first : first + span_east, second : second + span_north]
        total = total + within_layer[:, first : first + span_east, second : second + span_north] * (
            near - center
        )
    return center + NU_COEF * within_layer[:, 1:-1, 1:-1] * total


def level_below(values):
    return jnp.concatenate([values[..., 64:], values[..., -64:]], axis=-1)


def level_above_zero(values):
    return jnp.concatenate([jnp.zeros_like(values[..., :64]), values[..., :-64]], axis=-1)


def level_prefix(values, layer_tally):
    running = values
    reach = 1
    while reach < layer_tally:
        moved = jnp.concatenate(
            [jnp.zeros_like(running[..., : 64 * reach]), running[..., : -64 * reach]], axis=-1
        )
        running = running + moved
        reach = reach * 2
    return running


def spread_levels(column_values, layer_tally):
    return jnp.tile(column_values, (1, layer_tally))


def flat_mixer(temp_flat, kbg_flat):
    return (kbg_flat * (1.0 + 0.5 * jnp.tanh(temp_flat - level_below(temp_flat)))).astype(
        jnp.bfloat16
    )


def flat_validity(tile_amount, flat_width):
    levels = lax.broadcasted_iota(jnp.int32, (1, flat_width), 1) // 64
    valid = (levels < tile_amount[:, None]).astype(jnp.float32)
    active = (levels + 1 < tile_amount[:, None]).astype(jnp.float32)
    return (valid, active)


def totals(amounts_on_chip, valid):
    return jnp.sum(amounts_on_chip * valid[:, None], axis=(0, 2))


def column_step(
    temp_flat, kappa_flat, surface, valid, active, amounts_on_chip, reaction_rates, layer_tally
):
    atten = ATTEN_WATER + ATTEN_CHL * amounts_on_chip[:, 0]
    cumul = level_prefix(atten, layer_tally)
    top = surface * jnp.exp(-(cumul - atten))
    bottom = surface * jnp.exp(-cumul)
    heat = (valid * (top - bottom)).astype(jnp.bfloat16)
    growth = jnp.exp(GROWTH_TEMP * temp_flat.astype(jnp.float32)) * top / (top + 1.0)
    mixed = jnp.einsum(
        "rs,nsf->nrf", reaction_rates, amounts_on_chip, precision=lax.Precision.HIGHEST
    )
    flux = (kappa_flat.astype(jnp.float32) * active)[:, None] * (
        level_below(amounts_on_chip) - amounts_on_chip
    )
    new = amounts_on_chip + valid[:, None] * STEP_DT * (
        flux - level_above_zero(flux) + growth[:, None] * mixed
    )
    return (new, heat)


def plane_blocks(field, blocks_x, blocks_y):
    return (
        field.reshape(blocks_x, 8, blocks_y, 8)
        .transpose(0, 2, 1, 3)
        .reshape(blocks_x * blocks_y, 64)
    )


def on_device(
    thermal_anomaly,
    ambient_diffusion,
    solar_light,
    sea_tile_flags,
    flooded_layer_tally,
    tile_holder_rank,
    solute_amounts,
    reaction_rates,
):
    layer_tally = thermal_anomaly.shape[0]
    span_east = thermal_anomaly.shape[1]
    span_north = thermal_anomaly.shape[2]
    blocks_x = span_east // 8
    blocks_y = span_north // 8
    tile_summation = blocks_x * blocks_y
    flat_width = layer_tally * 64
    depth_block = (sea_tile_flags * flooded_layer_tally).reshape(tile_summation)
    cell_count = jnp.repeat(
        jnp.repeat(depth_block.reshape(blocks_x, blocks_y), 8, axis=0), 8, axis=1
    )
    level_idx = lax.broadcasted_iota(jnp.int32, (layer_tally, 1, 1), 0)
    within_layer = (level_idx < cell_count[None]).astype(jnp.float32)
    piled_tiles = jnp.stack([thermal_anomaly, within_layer])
    padded = with_halo(piled_tiles, (("gx", 2), ("gy", 3)), 1)
    advanced_verticals = masked_step(padded[0], padded[1])
    dispatched = advanced_verticals.astype(jnp.bfloat16)
    thermal_tiles = (
        dispatched.reshape(layer_tally, blocks_x, 8, blocks_y, 8)
        .transpose(1, 3, 0, 2, 4)
        .reshape(tile_summation, flat_width)
    )
    ambient_diffusion_tiles = plane_blocks(ambient_diffusion, blocks_x, blocks_y)
    shortwave_blocks = plane_blocks(solar_light, blocks_x, blocks_y)
    diffusion_each_tile = flat_mixer(
        thermal_tiles.astype(jnp.float32),
        spread_levels(ambient_diffusion_tiles.astype(jnp.float32), layer_tally),
    )
    payload = jnp.concatenate([thermal_tiles, diffusion_each_tile, shortwave_blocks], axis=1)
    holder_chip = tile_holder_rank.reshape(tile_summation)
    order = jnp.arange(tile_summation, dtype=jnp.int32)
    same = (holder_chip[:, None] == holder_chip[None, :]) & (order[None, :] < order[:, None])
    rank = jnp.sum(same.astype(jnp.int32), axis=1)
    position_summation = solute_amounts.shape[2]
    device_groups = lax.axis_size("gy")
    slot_limit = position_summation // device_groups
    target_owner = holder_chip * slot_limit + rank
    selection_mask = (
        lax.broadcasted_iota(jnp.int32, (position_summation, tile_summation), 0)
        == target_owner[None, :]
    )
    select_b = selection_mask.astype(jnp.bfloat16)
    packed = jnp.einsum("sb,bf->sf", select_b, payload, preferred_element_type=jnp.float32).astype(
        jnp.bfloat16
    )
    packed_count = jnp.sum(selection_mask.astype(jnp.int32) * depth_block[None, :], axis=1)
    arrived_tiles, received_count = (
        lax.all_to_all(
            packed.reshape(device_groups, slot_limit, packed.shape[1]),
            "gy",
            split_axis=0,
            concat_axis=0,
            tiled=True,
        ),
        lax.all_to_all(
            packed_count.reshape(device_groups, slot_limit),
            "gy",
            split_axis=0,
            concat_axis=0,
            tiled=True,
        ),
    )
    arrived_tiles = arrived_tiles.reshape(position_summation, arrived_tiles.shape[2])
    tile_amount = received_count.reshape(position_summation)
    thermal_at_position = arrived_tiles[:, :flat_width]
    diffusion_at_position = arrived_tiles[:, flat_width : 2 * flat_width]
    solar_at_position = arrived_tiles[:, 2 * flat_width :]
    surface = spread_levels(solar_at_position.astype(jnp.float32), layer_tally)
    amounts_on_chip = solute_amounts.reshape(
        position_summation, solute_amounts.shape[3], flat_width
    )
    valid, active = flat_validity(tile_amount, flat_width)
    old_local = totals(amounts_on_chip, valid)
    cells_local = jnp.sum(valid)
    old_total, cells = lax.psum((old_local, cells_local), ("gx", "gy"))
    new, heat = column_step(
        thermal_at_position,
        diffusion_at_position,
        surface,
        valid,
        active,
        amounts_on_chip,
        reaction_rates,
        layer_tally,
    )
    new_total = lax.psum(totals(new, valid), ("gx", "gy"))
    shift = (old_total - new_total) / jnp.maximum(cells, 1.0)
    solute_final = jnp.where(
        valid[:, None] > 0, new + shift[None, :, None], amounts_on_chip
    ).reshape(solute_amounts.shape)
    returned_blocks = lax.all_to_all(
        heat.reshape(device_groups, slot_limit, flat_width),
        "gy",
        split_axis=0,
        concat_axis=0,
        tiled=True,
    )
    returned_blocks = returned_blocks.reshape(position_summation, flat_width)
    heat_blocks = jnp.einsum(
        "sb,sf->bf", select_b, returned_blocks, preferred_element_type=jnp.float32
    )
    warming_each_site = (
        heat_blocks.reshape(blocks_x, blocks_y, layer_tally, 8, 8)
        .transpose(2, 0, 3, 1, 4)
        .reshape(layer_tally, span_east, span_north)
    )
    thermal_final = advanced_verticals + WARMING_SCALE * warming_each_site
    return (thermal_final, solute_final)


def solution(mesh):
    return jax.shard_map(
        on_device,
        mesh=mesh,
        in_specs=(
            P(None, "gx", "gy"),
            P("gx", "gy"),
            P("gx", "gy"),
            P("gx", "gy", None),
            P("gx", "gy", None),
            P("gx", "gy", None, None),
            P("gx", "gy", None, None, None),
            P(),
        ),
        out_specs=(P(None, "gx", "gy"), P("gx", "gy", None, None, None)),
        check_vma=False,
    )
```

profile of v0, /device:TPU:0, one launch (start us, length us, event | category | flops | bytes accessed | tf_op | source)
XLA Modules:
  0.0 186.1 jit_solution(9731067672512701590)
XLA Ops:
  0.6 0.9 convert_reduce_fusion
  1.6 0.7 multiply_add_fusion
  2.2 0.7 multiply_bitcast_fusion.1
  3.0 0.7 all_to_all.12
  3.7 7.3 %all-to-all-start = ((s32[8,1,16]{2,1,0:T(1,128)}), s32[8,1,16]{2,1,0:T(1,128)S(1)}, u32[]{:S(2)}, u32[]{:S(2)}) async-start(s32[8,1,16]{2,1,0:T(1,128)} %bitcast.10), calls=%async_computation | async-start | bytes 8192 | tf_op jit(solution)/shard_map/all_to_all | solution.py:178
  11.3 1.2 pad_maximum_fusion.1
  12.5 2.7 %copy.128 = f32[2,32,32,128]{1,3,2,0:T(8,128)} copy(f32[2,32,32,128]{3,2,1,0:T(8,128)S(1)} %pad_maximum_fusion.1) | data formatting | bytes 2097152 | tf_op jit(solution)/shard_map/stack | solution.py:137
  15.2 1.1 fusion.39
  16.3 1.6 collective-permute-start
  17.9 1.3 collective-permute-start.1
  19.2 4.8 %fusion.18 = f32[128,1,2048]{2,1,0:T(1,128)S(1)} fusion(f32[128,8,2048]{2,1,0:T(8,128)} %bitcast.79), kind=kLoop, calls=%fused_computation.37 | loop fusion | flops 524288 | bytes 2097152 | tf_op jit(solution)/shard_map/add | solution.py:88
  24.0 0.3 copy.161
  24.7 1.3 collective-permute-start.3
  25.9 4.5 %collective-permute-start.2 = (f32[2,32,34,1]{2,1,3,0:T(8,128)S(1)}, f32[2,32,34,1]{2,1,3,0:T(8,128)S(1)}, u32[]{:S(2)}, u32[]{:S(2)}) collective-permute-start(f32[2,32,34,1]{2,1,3,0:T(8,128)S(1)} %copy.131), channel_id=1, source_target_pairs={{0,1},{1,2},{2,3},{3,4},{4,5},{5,6},{6,7},{8,9},{9,10},{10,11},{11... | collective-permute-start | bytes 26120 | tf_op jit(solution)/shard_map/ppermute | solution.py:22
  30.5 0.5 pad_add_fusion.4
  31.3 0.7 reshape.245
  32.5 0.9 copy.134
  33.4 2.7 %pad_maximum_fusion = f32[2,32,34,130]{1,3,2,0:T(8,128)S(1)} fusion(f32[2,32,34,1]{1,3,2,0:T(1,128)S(1)} %copy.134, f32[2,32,1,128]{1,3,2,0:T(8,128)S(1)} %collective-permute-done.1, f32[2,32,32,128]{1,3,2,0:T(8,128)} %copy.128, f32[2,32,1,128]{1,3,2,0:T(8,128)S(1)} %collective-permute-done, f32[2,32,34,1]{1,3,2,0:T(1,128)S(1)} %copy.133), kind=kLoop, calls=%fused_computation.9 | loop fusion | flops 1131520 | bytes 2263040 | tf_op jit(solution)/shard_map/concatenate | solution.py:20
  36.1 0.3 slice_bitcast_fusion
  36.4 3.6 %fusion.37 = (bf16[32,32,128]{0,2,1:T(8,128)(2,1)}, f32[32,32,128]{0,2,1:T(8,128)}) fusion(f32[32,34,130]{0,2,1:T(8,128)S(1)} %get-tuple-element.24, f32[32,34,130]{0,2,1:T(8,128)S(1)} %get-tuple-element.23), kind=kLoop, calls=%fused_computation.87 | loop fusion | flops 1966080 | bytes 6029312 | tf_op jit(solution)/shard_map/convert_element_type | solution.py:140
  40.0 4.9 %copy.136 = bf16[4,16,32,8,8]{1,0,4,3,2:T(4,128)(2,1)S(1)} copy(bf16[4,16,32,8,8]{2,4,1,3,0:T(8,128)(2,1)} %bitcast.87) | data formatting | bytes 524288 | tf_op jit(solution)/shard_map/transpose | solution.py:143
  45.0 1.8 reshape.243
  46.7 0.8 slice.135
  47.5 1.1 slice.134
  48.7 0.3 fusion.23
  48.9 1.5 convolution_convert_fusion
  50.4 2.5 %copy.139 = bf16[128,4160]{1,0:T(8,128)(2,1)} copy(bf16[128,4160]{0,1:T(8,128)(2,1)} %convolution_convert_fusion) | data formatting | bytes 2129920 | tf_op jit(solution)/shard_map/convert_element_type | solution.py:166
  53.0 6.3 %all-to-all-start.1 = ((bf16[8,16,4160]{2,1,0:T(8,128)(2,1)}), bf16[8,16,4160]{2,1,0:T(8,128)(2,1)}, u32[]{:S(2)}, u32[]{:S(2)}) async-start(bf16[8,16,4160]{2,1,0:T(8,128)(2,1)} %bitcast.86), calls=%async_computation.1 | async-start | bytes 2162688 | tf_op jit(solution)/shard_map/all_to_all | solution.py:171
  59.4 2.1 %slice.145 = f32[128,8,64]{2,1,0:T(8,128)} slice(f32[128,8,2048]{2,1,0:T(8,128)} %bitcast.80), slice={[0:128], [0:8], [1984:2048]} | slice | bytes 524288 | tf_op jit(solution)/shard_map/slice | solution.py:45
  61.5 9.0 %slice.144 = f32[128,8,1984]{2,1,0:T(8,128)} slice(f32[128,8,2048]{2,1,0:T(8,128)} %bitcast.81), slice={[0:128], [0:8], [64:2048]} | slice | bytes 16252928 | tf_op jit(solution)/shard_map/slice | solution.py:45
  70.9 0.8 slice.142
  71.8 0.5 broadcast.192
  72.3 0.6 reduce.7
  72.9 1.3 fusion.25
  74.2 12.9 %all-to-all-done.1 = bf16[8,16,4160]{2,1,0:T(8,128)(2,1)} async-done(((bf16[8,16,4160]{2,1,0:T(8,128)(2,1)}), bf16[8,16,4160]{2,1,0:T(8,128)(2,1)}, u32[]{:S(2)}, u32[]{:S(2)}) %all-to-all-start.1) | async-done | bytes 1064992 | tf_op jit(solution)/shard_map/all_to_all | solution.py:171
  87.1 0.8 slice.136
  88.1 1.4 copy.141
  89.5 4.6 %add_divide_fusion = (f32[128,2048]{1,0:T(8,128)S(1)}, bf16[128,2048]{1,0:T(8,128)(2,1)}, f32[128,2048]{1,0:T(8,128)}, f32[]{:T(128)}, f32[128,2048]{1,0:T(8,128)}) fusion(f32[128,2048]{1,0:T(8,128)} %copy.141, f32[128,2048]{1,0:T(8,128)S(1)} %pad_add_fusion.1, f32[128,1024]{1,0:T(8,128)} %slice.142, bf16[128,4160]{1,0:T(8,128)(2,1)} %bitcast.17, ...), kind=kLoop, calls=%fused_computation.46 | loop fusion | flops 5505023 | bytes 8405508 | tf_op jit(solution)/shard_map/div | solution.py:93
  94.1 3.7 %all-to-all-start.2 = ((bf16[8,16,2048]{2,1,0:T(8,128)(2,1)}), bf16[8,16,2048]{2,1,0:T(8,128)(2,1)S(1)}, u32[]{:S(2)}, u32[]{:S(2)}) async-start(bf16[8,16,2048]{2,1,0:T(8,128)(2,1)} %bitcast.90), calls=%async_computation.2 | async-start | bytes 1048576 | tf_op jit(solution)/shard_map/all_to_all | solution.py:214
  97.9 11.1 %fusion = f32[128,8,2048]{2,1,0:T(8,128)} fusion(f32[128,8,64]{2,1,0:T(8,128)} %slice.145, f32[128,8,1984]{2,1,0:T(8,128)} %slice.144, f32[128,2048]{1,0:T(8,128)} %get-tuple-element.31, f32[1,1,128,8,2048]{4,3,2,1,0:T(8,128)} %param.14), kind=kLoop, calls=%fused_computation.1 | loop fusion | flops 6291456 | bytes 26214400 | tf_op jit(solution)/shard_map/mul | solution.py:97
  109.1 21.6 %multiply_reduce_fusion = (f32[8]{0:T(128)S(1)}, f32[8]{0:T(128)S(1)}, f32[128,8,2048]{2,1,0:T(8,128)}) fusion(f32[128,2048]{1,0:T(8,128)S(1)} %copy-done.7, f32[1,1,128,8,2048]{4,3,2,1,0:T(8,128)S(1)} %bitcast.83, f32[8,8]{1,0:T(8,128)S(1)} %copy-done, f32[128,2048]{1,0:T(8,128)S(1)} %get-tuple-element.29, f32[128,8,2048]{2,1,0:T(8,128)} %fusion, ...), kind=kOutput, calls=%fused_computation.6 | convolution fusion | flops 220200944 | bytes 36438336 | tf_op jit(solution)/shard_map/rs,nsf->nrf/dot_general | solution.py:94
  130.8 40.8 %all-reduce.6 = (f32[8]{0:T(128)S(1)}, f32[8]{0:T(128)S(1)}, f32[]{:T(128)}) all-reduce(f32[8]{0:T(128)S(1)} %get-tuple-element.17, f32[8]{0:T(128)S(1)} %get-tuple-element.16, f32[]{:T(128)} %get-tuple-element.32), channel_id=1, replica_groups=mesh['gx'=4,'gy'=8] {'gx','gy'}, use_global_device_ids=true, to_apply=%region_3.4 | all-reduce | flops 17 | bytes 136 | tf_op jit(solution)/shard_map/psum | solution.py:198
  172.2 9.3 %select_bitcast_fusion = f32[1,1,128,8,2048]{4,3,2,1,0:T(8,128)} fusion(f32[128,8,2048]{2,1,0:T(8,128)} %get-tuple-element.38, f32[8]{0:T(128)S(1)} %subtract_divide_fusion, pred[128,2048]{1,0:T(8,128)(4,1)S(1)} %get-tuple-element.34, f32[1,1,128,8,2048]{4,3,2,1,0:T(8,128)} %param.14), kind=kLoop, calls=%fused_computation.5 | loop fusion | flops 4194304 | bytes 25428000 | tf_op jit(solution)/shard_map/reshape | solution.py:213
  181.5 0.3 copy.143
  181.8 1.0 multiply_bitcast_fusion
  182.8 0.9 copy.145
  183.7 0.7 copy-done.4
  184.6 1.5 copy.146
  (62 shorter events, 2.7 us)
Async XLA Ops:
  0.6 108.4 %copy-start = (f32[8,8]{1,0:T(8,128)S(1)}, f32[8,8]{1,0:T(8,128)}, u32[]{:S(2)}) copy-start(f32[8,8]{1,0:T(8,128)} %param.15) | copy-start | bytes 772
  3.7 49.3 %all-to-all-start = ((s32[8,1,16]{2,1,0:T(1,128)}), s32[8,1,16]{2,1,0:T(1,128)S(1)}, u32[]{:S(2)}, u32[]{:S(2)}) async-start(s32[8,1,16]{2,1,0:T(1,128)} %bitcast.10), calls=%async_computation | async-start | bytes 8192 | tf_op jit(solution)/shard_map/all_to_all | solution.py:178
  15.2 9.2 %copy-start.1 = (f32[2,32,32,128]{1,3,2,0:T(8,128)S(1)}, f32[2,32,32,128]{1,3,2,0:T(8,128)}, u32[]{:S(2)}) copy-start(f32[2,32,32,128]{1,3,2,0:T(8,128)} %copy.128) | copy-start | bytes 3145732
  16.3 8.0 %collective-permute-start = (f32[2,32,1,128]{1,3,2,0:T(8,128)S(1)}, f32[2,32,1,128]{1,3,2,0:T(8,128)S(1)}, u32[]{:S(2)}, u32[]{:S(2)}) collective-permute-start(f32[2,32,1,128]{1,3,2,0:T(8,128)S(1)} %get-tuple-element.27), channel_id=1, source_target_pairs={{0,8},{8,16},{16,24},{1,9},{9,17},{17,25},{2,10},{10,18},{18,26},{... | collective-permute-start | bytes 98312 | tf_op jit(solution)/shard_map/ppermute | solution.py:22
  17.9 6.4 %collective-permute-start.1 = (f32[2,32,1,128]{1,3,2,0:T(8,128)S(1)}, f32[2,32,1,128]{1,3,2,0:T(8,128)S(1)}, u32[]{:S(2)}, u32[]{:S(2)}) collective-permute-start(f32[2,32,1,128]{1,3,2,0:T(8,128)S(1)} %get-tuple-element.28), channel_id=1, source_target_pairs={{8,0},{16,8},{24,16},{9,1},{17,9},{25,17},{10,2},{18,10},{26,18},{... | collective-permute-start | bytes 98312 | tf_op jit(solution)/shard_map/ppermute | solution.py:24
  24.5 6.5 %copy-start.9 = (bf16[32,128]{1,0:T(8,128)(2,1)S(1)}, bf16[32,128]{1,0:T(8,128)(2,1)}, u32[]{:S(2)}) copy-start(bf16[32,128]{1,0:T(8,128)(2,1)} %param.10) | copy-start | bytes 24580
  24.5 7.6 %copy-start.10 = (bf16[32,128]{1,0:T(8,128)(2,1)S(1)}, bf16[32,128]{1,0:T(8,128)(2,1)}, u32[]{:S(2)}) copy-start(bf16[32,128]{1,0:T(8,128)(2,1)} %param.9) | copy-start | bytes 24580
  24.7 7.8 %collective-permute-start.3 = (f32[2,32,34,1]{2,1,3,0:T(8,128)S(1)}, f32[2,32,34,1]{2,1,3,0:T(8,128)}, u32[]{:S(2)}, u32[]{:S(2)}) collective-permute-start(f32[2,32,34,1]{2,1,3,0:T(8,128)S(1)} %copy.132), channel_id=1, source_target_pairs={{1,0},{2,1},{3,2},{4,3},{5,4},{6,5},{7,6},{9,8},{10,9},{11,10},{12... | collective-permute-start | bytes 26120 | tf_op jit(solution)/shard_map/ppermute | solution.py:24
  25.9 7.4 %collective-permute-start.2 = (f32[2,32,34,1]{2,1,3,0:T(8,128)S(1)}, f32[2,32,34,1]{2,1,3,0:T(8,128)S(1)}, u32[]{:S(2)}, u32[]{:S(2)}) collective-permute-start(f32[2,32,34,1]{2,1,3,0:T(8,128)S(1)} %copy.131), channel_id=1, source_target_pairs={{0,1},{1,2},{2,3},{3,4},{4,5},{5,6},{6,7},{8,9},{9,10},{10,11},{11... | collective-permute-start | bytes 26120 | tf_op jit(solution)/shard_map/ppermute | solution.py:22
  31.0 5.1 %copy-start.2 = (f32[128,2048]{1,0:T(8,128)}, f32[128,2048]{1,0:T(8,128)S(1)}, u32[]{:S(2)}) copy-start(f32[128,2048]{1,0:T(8,128)S(1)} %pad_add_fusion.4) | copy-start | bytes 3145732
  46.7 1.9 %copy-start.5 = (bf16[64,2048]{0,1:T(8,128)(2,1)S(1)}, bf16[64,2048]{0,1:T(8,128)(2,1)}, u32[]{:S(2)}) copy-start(bf16[64,2048]{0,1:T(8,128)(2,1)} %reshape.243) | copy-start | bytes 786436
  46.7 2.2 %copy-start.8 = (bf16[64,64]{0,1:T(8,128)(2,1)S(1)}, bf16[64,64]{0,1:T(8,128)(2,1)}, u32[]{:S(2)}) copy-start(bf16[64,64]{0,1:T(8,128)(2,1)} %reshape.245) | copy-start | bytes 24580
  50.4 8.9 %copy-start.3 = (f32[128,2048]{1,0:T(8,128)S(1)}, f32[128,2048]{1,0:T(8,128)}, u32[]{:S(2)}) copy-start(f32[128,2048]{1,0:T(8,128)} %copy-done.2) | copy-start | bytes 3145732
  50.4 8.9 %slice-start.2 = ((f32[128,2048]{1,0:T(8,128)}), f32[128,1920]{1,0:T(8,128)S(1)}, s32[]{:S(2)}) async-start(f32[128,2048]{1,0:T(8,128)} %copy-done.2), calls=%async_computation.5 | async-start | bytes 1966080 | tf_op jit(solution)/shard_map/slice | solution.py:57
  53.0 34.2 %all-to-all-start.1 = ((bf16[8,16,4160]{2,1,0:T(8,128)(2,1)}), bf16[8,16,4160]{2,1,0:T(8,128)(2,1)}, u32[]{:S(2)}, u32[]{:S(2)}) async-start(bf16[8,16,4160]{2,1,0:T(8,128)(2,1)} %bitcast.86), calls=%async_computation.1 | async-start | bytes 2162688 | tf_op jit(solution)/shard_map/all_to_all | solution.py:171
  94.1 87.4 %all-to-all-start.2 = ((bf16[8,16,2048]{2,1,0:T(8,128)(2,1)}), bf16[8,16,2048]{2,1,0:T(8,128)(2,1)S(1)}, u32[]{:S(2)}, u32[]{:S(2)}) async-start(bf16[8,16,2048]{2,1,0:T(8,128)(2,1)} %bitcast.90), calls=%async_computation.2 | async-start | bytes 1048576 | tf_op jit(solution)/shard_map/all_to_all | solution.py:214
  97.8 11.2 %slice-start = ((s8[8388608]{0:T(1024)(128)(4,1)}), s8[4194304]{0:T(1024)(128)(4,1)S(1)}, s32[]{:S(2)}) async-start(s8[8388608]{0:T(1024)(128)(4,1)} %bitcast.82), calls=%async_computation.3 | async-start | bytes 8388608
  97.8 11.2 %slice-start.1 = ((s8[8388608]{0:T(1024)(128)(4,1)}), s8[4194304]{0:T(1024)(128)(4,1)S(1)}, s32[]{:S(2)}) async-start(s8[8388608]{0:T(1024)(128)(4,1)} %bitcast.82), calls=%async_computation.4 | async-start | bytes 8388608
  97.9 11.2 %copy-start.6 = (f32[128,2048]{1,0:T(8,128)S(1)}, f32[128,2048]{1,0:T(8,128)}, u32[]{:S(2)}) copy-start(f32[128,2048]{1,0:T(8,128)} %get-tuple-element.33) | copy-start | bytes 3145732
  97.9 11.3 %copy-start.7 = (f32[128,2048]{1,0:T(8,128)S(1)}, f32[128,2048]{1,0:T(8,128)}, u32[]{:S(2)}) copy-start(f32[128,2048]{1,0:T(8,128)} %get-tuple-element.35) | copy-start | bytes 3145732
  182.8 1.6 copy-start.4
where the time goes:
time: 187 us; the launch traced here: 186 us
  other arithmetic  43 us (23%)
  blocking collectives  40.8 us (22%)
  local copies, waits for them, and re-layouts  37.5 us (20%)
  starting transfers between devices  26.1 us (14%)
  matrix products  24.1 us (13%)
  waiting for transfers between devices  12.9 us (7%)
    psum x1, blocking collectives, on_device(): old_total, cells = lax.psum((old_local, cells_local), ('gx', 'gy'))  40.8 us
    dot_general x1, matrix products, column_step(): jnp.einsum('rs,nsf->nrf', reaction_rates, amounts_on_chip, precision=lax....  21.6 us
    slice x4, local copies, waits for them, and re-layouts, level_below(): return jnp.concatenate([values[..., 64:], values[..., -64:]], axis=-1)  13 us
    all_to_all x1, waiting for transfers between devices, on_device(): lax.all_to_all(packed.reshape(device_groups, slot_limit, packed.shape[1])...  12.9 us
    mul x1, other arithmetic, column_step(): (kappa_flat.astype(jnp.float32) * active)[:, None]  11.1 us
    reshape x1, other arithmetic, on_device(): solute_final = jnp.where(valid[:, None] > 0, new + shift[None, :, None],...  9.28 us
    all_to_all x1, starting transfers between devices, on_device(): lax.all_to_all(packed_count.reshape(device_groups, slot_limit), 'gy', spl...  7.28 us
    all_to_all x1, starting transfers between devices, on_device(): lax.all_to_all(packed.reshape(device_groups, slot_limit, packed.shape[1])...  6.32 us
  transfers between devices with their start and end apart: 7, of which 1 were waited for; matrix products, arithmetic and copies ran while one was open for 48% of the time, Pallas kernels for 0%

commit v1 on v0

--- a/solution.py
+++ b/solution.py
@@ -195,7 +195,7 @@
     valid, active = flat_validity(tile_amount, flat_width)
     old_local = totals(amounts_on_chip, valid)
     cells_local = jnp.sum(valid)
-    old_total, cells = lax.psum((old_local, cells_local), ("gx", "gy"))
+    old_total, cells = lax.psum(lax.psum((old_local, cells_local), "gy"), "gx")
     new, heat = column_step(
         thermal_at_position,
         diffusion_at_position,

time: 187 us -> 215 us (1.15)
  blocking collectives: 40.8 us -> 68.5 us
    psum x1 -> x3, blocking collectives: 40.8 us -> 68.5 us  [the longest x1 40.3 us: on_device(): new_total = lax.psum(totals(new, valid), ('gx', 'gy'))]
  transfers between devices with their start and end apart: 7 -> 7, of which waited for: 1 -> 1; matrix products, arithmetic and copies ran while one was open for 48% -> 42% of each run, Pallas kernels for 0% -> 0%
where the time goes in v1:
time: 215 us; the launch traced here: 214 us
  blocking collectives  68.5 us (32%)
  other arithmetic  43.1 us (20%)
  local copies, waits for them, and re-layouts  37.4 us (17%)
  starting transfers between devices  26.1 us (12%)
  matrix products  24.1 us (11%)
  waiting for transfers between devices  12.8 us (6%)
    psum x1, blocking collectives, on_device(): new_total = lax.psum(totals(new, valid), ('gx', 'gy'))  40.3 us
    psum x2, blocking collectives, on_device(): old_total, cells = lax.psum(lax.psum((old_local, cells_local), 'gy'), 'gx')  28.2 us
    dot_general x1, matrix products, column_step(): jnp.einsum('rs,nsf->nrf', reaction_rates, amounts_on_chip, precision=lax....  21.6 us
    slice x4, local copies, waits for them, and re-layouts, level_below(): return jnp.concatenate([values[..., 64:], values[..., -64:]], axis=-1)  12.9 us
    all_to_all x1, waiting for transfers between devices, on_device(): lax.all_to_all(packed.reshape(device_groups, slot_limit, packed.shape[1])...  12.8 us
    mul x1, other arithmetic, column_step(): (kappa_flat.astype(jnp.float32) * active)[:, None]  11.1 us
    reshape x1, other arithmetic, on_device(): solute_final = jnp.where(valid[:, None] > 0, new + shift[None, :, None],...  9.28 us
    all_to_all x1, starting transfers between devices, on_device(): lax.all_to_all(packed_count.reshape(device_groups, slot_limit), 'gy', spl...  7.28 us
  transfers between devices with their start and end apart: 7, of which 1 were waited for; matrix products, arithmetic and copies ran while one was open for 42% of the time, Pallas kernels for 0%

profile of v1, /device:TPU:0, one launch (start us, length us, event | category | flops | bytes accessed | tf_op | source)
XLA Modules:
  0.0 213.6 jit_solution(17995508560210853300)
XLA Ops:
  0.6 0.9 convert_reduce_fusion
  1.6 0.7 multiply_add_fusion
  2.2 0.7 multiply_bitcast_fusion.1
  3.0 0.7 all_to_all.12
  3.7 7.3 %all-to-all-start = ((s32[8,1,16]{2,1,0:T(1,128)}), s32[8,1,16]{2,1,0:T(1,128)S(1)}, u32[]{:S(2)}, u32[]{:S(2)}) async-start(s32[8,1,16]{2,1,0:T(1,128)} %bitcast.10), calls=%async_computation | async-start | bytes 8192 | tf_op jit(solution)/shard_map/all_to_all | solution.py:178
  11.3 1.2 pad_maximum_fusion.1
  12.5 2.7 %copy.128 = f32[2,32,32,128]{1,3,2,0:T(8,128)} copy(f32[2,32,32,128]{3,2,1,0:T(8,128)S(1)} %pad_maximum_fusion.1) | data formatting | bytes 2097152 | tf_op jit(solution)/shard_map/stack | solution.py:137
  15.2 1.1 fusion.39
  16.3 1.6 collective-permute-start
  17.9 1.3 collective-permute-start.1
  19.2 4.8 %fusion.18 = f32[128,1,2048]{2,1,0:T(1,128)S(1)} fusion(f32[128,8,2048]{2,1,0:T(8,128)} %bitcast.79), kind=kLoop, calls=%fused_computation.37 | loop fusion | flops 524288 | bytes 2097152 | tf_op jit(solution)/shard_map/add | solution.py:88
  24.0 0.3 copy.161
  24.6 1.3 collective-permute-start.3
  25.9 4.5 %collective-permute-start.2 = (f32[2,32,34,1]{2,1,3,0:T(8,128)S(1)}, f32[2,32,34,1]{2,1,3,0:T(8,128)S(1)}, u32[]{:S(2)}, u32[]{:S(2)}) collective-permute-start(f32[2,32,34,1]{2,1,3,0:T(8,128)S(1)} %copy.131), channel_id=1, source_target_pairs={{0,1},{1,2},{2,3},{3,4},{4,5},{5,6},{6,7},{8,9},{9,10},{10,11},{11... | collective-permute-start | bytes 26120 | tf_op jit(solution)/shard_map/ppermute | solution.py:22
  30.5 0.5 pad_add_fusion.4
  31.3 0.7 reshape.245
  32.5 0.9 copy.134
  33.4 2.7 %pad_maximum_fusion = f32[2,32,34,130]{1,3,2,0:T(8,128)S(1)} fusion(f32[2,32,34,1]{1,3,2,0:T(1,128)S(1)} %copy.134, f32[2,32,1,128]{1,3,2,0:T(8,128)S(1)} %collective-permute-done.1, f32[2,32,32,128]{1,3,2,0:T(8,128)} %copy.128, f32[2,32,1,128]{1,3,2,0:T(8,128)S(1)} %collective-permute-done, f32[2,32,34,1]{1,3,2,0:T(1,128)S(1)} %copy.133), kind=kLoop, calls=%fused_computation.9 | loop fusion | flops 1131520 | bytes 2263040 | tf_op jit(solution)/shard_map/concatenate | solution.py:20
  36.1 0.3 slice_bitcast_fusion
  36.4 3.6 %fusion.37 = (bf16[32,32,128]{0,2,1:T(8,128)(2,1)}, f32[32,32,128]{0,2,1:T(8,128)}) fusion(f32[32,34,130]{0,2,1:T(8,128)S(1)} %get-tuple-element.25, f32[32,34,130]{0,2,1:T(8,128)S(1)} %get-tuple-element.24), kind=kLoop, calls=%fused_computation.87 | loop fusion | flops 1966080 | bytes 6029312 | tf_op jit(solution)/shard_map/convert_element_type | solution.py:140
  40.0 4.9 %copy.136 = bf16[4,16,32,8,8]{1,0,4,3,2:T(4,128)(2,1)S(1)} copy(bf16[4,16,32,8,8]{2,4,1,3,0:T(8,128)(2,1)} %bitcast.87) | data formatting | bytes 524288 | tf_op jit(solution)/shard_map/transpose | solution.py:143
  45.0 1.8 reshape.243
  46.7 0.8 slice.135
  47.5 1.1 slice.134
  48.9 1.5 convolution_convert_fusion
  50.4 2.5 %copy.139 = bf16[128,4160]{1,0:T(8,128)(2,1)} copy(bf16[128,4160]{0,1:T(8,128)(2,1)} %convolution_convert_fusion) | data formatting | bytes 2129920 | tf_op jit(solution)/shard_map/convert_element_type | solution.py:166
  53.0 6.3 %all-to-all-start.1 = ((bf16[8,16,4160]{2,1,0:T(8,128)(2,1)}), bf16[8,16,4160]{2,1,0:T(8,128)(2,1)}, u32[]{:S(2)}, u32[]{:S(2)}) async-start(bf16[8,16,4160]{2,1,0:T(8,128)(2,1)} %bitcast.86), calls=%async_computation.1 | async-start | bytes 2162688 | tf_op jit(solution)/shard_map/all_to_all | solution.py:171
  59.4 2.0 slice.145
  61.4 9.0 %slice.144 = f32[128,8,1984]{2,1,0:T(8,128)} slice(f32[128,8,2048]{2,1,0:T(8,128)} %bitcast.81), slice={[0:128], [0:8], [64:2048]} | slice | bytes 16252928 | tf_op jit(solution)/shard_map/slice | solution.py:45
  70.8 0.8 slice.142
  71.7 0.5 broadcast.192
  72.3 0.6 reduce.7
  73.0 1.3 fusion.25
  74.3 12.8 %all-to-all-done.1 = bf16[8,16,4160]{2,1,0:T(8,128)(2,1)} async-done(((bf16[8,16,4160]{2,1,0:T(8,128)(2,1)}), bf16[8,16,4160]{2,1,0:T(8,128)(2,1)}, u32[]{:S(2)}, u32[]{:S(2)}) %all-to-all-start.1) | async-done | bytes 1064992 | tf_op jit(solution)/shard_map/all_to_all | solution.py:171
  87.1 0.8 slice.136
  88.1 1.4 copy.141
  89.4 4.6 %add_divide_fusion = (f32[128,2048]{1,0:T(8,128)S(1)}, bf16[128,2048]{1,0:T(8,128)(2,1)}, f32[128,2048]{1,0:T(8,128)}, f32[]{:T(128)}, f32[128,2048]{1,0:T(8,128)}) fusion(f32[128,2048]{1,0:T(8,128)} %copy.141, f32[128,2048]{1,0:T(8,128)S(1)} %pad_add_fusion.1, f32[128,1024]{1,0:T(8,128)} %slice.142, bf16[128,4160]{1,0:T(8,128)(2,1)} %bitcast.17, ...), kind=kLoop, calls=%fused_computation.46 | loop fusion | flops 5505023 | bytes 8405508 | tf_op jit(solution)/shard_map/div | solution.py:93
  94.1 3.8 %all-to-all-start.2 = ((bf16[8,16,2048]{2,1,0:T(8,128)(2,1)}), bf16[8,16,2048]{2,1,0:T(8,128)(2,1)S(1)}, u32[]{:S(2)}, u32[]{:S(2)}) async-start(bf16[8,16,2048]{2,1,0:T(8,128)(2,1)} %bitcast.90), calls=%async_computation.2 | async-start | bytes 1048576 | tf_op jit(solution)/shard_map/all_to_all | solution.py:214
  97.8 11.1 %fusion = f32[128,8,2048]{2,1,0:T(8,128)} fusion(f32[128,8,64]{2,1,0:T(8,128)} %slice.145, f32[128,8,1984]{2,1,0:T(8,128)} %slice.144, f32[128,2048]{1,0:T(8,128)} %get-tuple-element.32, f32[1,1,128,8,2048]{4,3,2,1,0:T(8,128)} %param.14), kind=kLoop, calls=%fused_computation.1 | loop fusion | flops 6291456 | bytes 26214400 | tf_op jit(solution)/shard_map/mul | solution.py:97
  109.0 21.6 %multiply_reduce_fusion = (f32[8]{0:T(128)S(1)}, f32[8]{0:T(128)S(1)}, f32[128,8,2048]{2,1,0:T(8,128)}) fusion(f32[128,2048]{1,0:T(8,128)S(1)} %copy-done.7, f32[1,1,128,8,2048]{4,3,2,1,0:T(8,128)S(1)} %bitcast.83, f32[8,8]{1,0:T(8,128)S(1)} %copy-done, f32[128,2048]{1,0:T(8,128)S(1)} %get-tuple-element.30, f32[128,8,2048]{2,1,0:T(8,128)} %fusion, ...), kind=kOutput, calls=%fused_computation.6 | convolution fusion | flops 220200944 | bytes 36438336 | tf_op jit(solution)/shard_map/rs,nsf->nrf/dot_general | solution.py:94
  130.6 40.3 %psum.37 = f32[8]{0:T(128)S(1)} all-reduce(f32[8]{0:T(128)S(1)} %get-tuple-element.16), channel_id=1, replica_groups=mesh['gx'=4,'gy'=8] {'gx','gy'}, use_global_device_ids=true, to_apply=%region_6.7 | all-reduce | flops 8 | bytes 64 | tf_op jit(solution)/shard_map/psum | solution.py:209
  170.9 21.7 %all-reduce.6 = (f32[8]{0:T(128)S(1)}, f32[]{:T(128)}) all-reduce(f32[8]{0:T(128)S(1)} %get-tuple-element.17, f32[]{:T(128)} %get-tuple-element.33), channel_id=1, replica_groups=mesh['gx'=4,'gy'=8] {'gy'}, use_global_device_ids=true, to_apply=%region_3.4 | all-reduce | flops 9 | bytes 72 | tf_op jit(solution)/shard_map/psum | solution.py:198
  192.6 6.5 %all-reduce.7 = (f32[8]{0:T(128)S(1)}, f32[]{:T(128)}) all-reduce(f32[8]{0:T(128)S(1)} %get-tuple-element.18, f32[]{:T(128)} %get-tuple-element.19), channel_id=1, replica_groups=mesh['gx'=4,'gy'=8] {'gx'}, use_global_device_ids=true, to_apply=%region_4.5 | all-reduce | flops 9 | bytes 72 | tf_op jit(solution)/shard_map/psum | solution.py:198
  199.7 9.3 %select_bitcast_fusion = f32[1,1,128,8,2048]{4,3,2,1,0:T(8,128)} fusion(f32[128,8,2048]{2,1,0:T(8,128)} %get-tuple-element.39, f32[8]{0:T(128)S(1)} %subtract_divide_fusion, pred[128,2048]{1,0:T(8,128)(4,1)S(1)} %get-tuple-element.35, f32[1,1,128,8,2048]{4,3,2,1,0:T(8,128)} %param.14), kind=kLoop, calls=%fused_computation.5 | loop fusion | flops 4194304 | bytes 25428000 | tf_op jit(solution)/shard_map/reshape | solution.py:213
  209.3 1.0 multiply_bitcast_fusion
  210.3 0.9 copy.145
  211.2 0.7 copy-done.4
  212.2 1.5 copy.146
  (64 shorter events, 3.2 us)
Async XLA Ops:
  0.6 108.3 %copy-start = (f32[8,8]{1,0:T(8,128)S(1)}, f32[8,8]{1,0:T(8,128)}, u32[]{:S(2)}) copy-start(f32[8,8]{1,0:T(8,128)} %param.15) | copy-start | bytes 772
  3.7 49.3 %all-to-all-start = ((s32[8,1,16]{2,1,0:T(1,128)}), s32[8,1,16]{2,1,0:T(1,128)S(1)}, u32[]{:S(2)}, u32[]{:S(2)}) async-start(s32[8,1,16]{2,1,0:T(1,128)} %bitcast.10), calls=%async_computation | async-start | bytes 8192 | tf_op jit(solution)/shard_map/all_to_all | solution.py:178
  15.2 9.2 %copy-start.1 = (f32[2,32,32,128]{1,3,2,0:T(8,128)S(1)}, f32[2,32,32,128]{1,3,2,0:T(8,128)}, u32[]{:S(2)}) copy-start(f32[2,32,32,128]{1,3,2,0:T(8,128)} %copy.128) | copy-start | bytes 3145732
  16.3 8.0 %collective-permute-start = (f32[2,32,1,128]{1,3,2,0:T(8,128)S(1)}, f32[2,32,1,128]{1,3,2,0:T(8,128)S(1)}, u32[]{:S(2)}, u32[]{:S(2)}) collective-permute-start(f32[2,32,1,128]{1,3,2,0:T(8,128)S(1)} %get-tuple-element.28), channel_id=1, source_target_pairs={{0,8},{8,16},{16,24},{1,9},{9,17},{17,25},{2,10},{10,18},{18,26},{... | collective-permute-start | bytes 98312 | tf_op jit(solution)/shard_map/ppermute | solution.py:22
  17.9 6.4 %collective-permute-start.1 = (f32[2,32,1,128]{1,3,2,0:T(8,128)S(1)}, f32[2,32,1,128]{1,3,2,0:T(8,128)S(1)}, u32[]{:S(2)}, u32[]{:S(2)}) collective-permute-start(f32[2,32,1,128]{1,3,2,0:T(8,128)S(1)} %get-tuple-element.29), channel_id=1, source_target_pairs={{8,0},{16,8},{24,16},{9,1},{17,9},{25,17},{10,2},{18,10},{26,18},{... | collective-permute-start | bytes 98312 | tf_op jit(solution)/shard_map/ppermute | solution.py:24
  24.4 6.5 %copy-start.9 = (bf16[32,128]{1,0:T(8,128)(2,1)S(1)}, bf16[32,128]{1,0:T(8,128)(2,1)}, u32[]{:S(2)}) copy-start(bf16[32,128]{1,0:T(8,128)(2,1)} %param.10) | copy-start | bytes 24580
  24.5 7.6 %copy-start.10 = (bf16[32,128]{1,0:T(8,128)(2,1)S(1)}, bf16[32,128]{1,0:T(8,128)(2,1)}, u32[]{:S(2)}) copy-start(bf16[32,128]{1,0:T(8,128)(2,1)} %param.9) | copy-start | bytes 24580
  24.6 7.8 %collective-permute-start.3 = (f32[2,32,34,1]{2,1,3,0:T(8,128)S(1)}, f32[2,32,34,1]{2,1,3,0:T(8,128)}, u32[]{:S(2)}, u32[]{:S(2)}) collective-permute-start(f32[2,32,34,1]{2,1,3,0:T(8,128)S(1)} %copy.132), channel_id=1, source_target_pairs={{1,0},{2,1},{3,2},{4,3},{5,4},{6,5},{7,6},{9,8},{10,9},{11,10},{12... | collective-permute-start | bytes 26120 | tf_op jit(solution)/shard_map/ppermute | solution.py:24
  25.9 7.4 %collective-permute-start.2 = (f32[2,32,34,1]{2,1,3,0:T(8,128)S(1)}, f32[2,32,34,1]{2,1,3,0:T(8,128)S(1)}, u32[]{:S(2)}, u32[]{:S(2)}) collective-permute-start(f32[2,32,34,1]{2,1,3,0:T(8,128)S(1)} %copy.131), channel_id=1, source_target_pairs={{0,1},{1,2},{2,3},{3,4},{4,5},{5,6},{6,7},{8,9},{9,10},{10,11},{11... | collective-permute-start | bytes 26120 | tf_op jit(solution)/shard_map/ppermute | solution.py:22
  31.0 5.1 %copy-start.2 = (f32[128,2048]{1,0:T(8,128)}, f32[128,2048]{1,0:T(8,128)S(1)}, u32[]{:S(2)}) copy-start(f32[128,2048]{1,0:T(8,128)S(1)} %pad_add_fusion.4) | copy-start | bytes 3145732
  46.7 1.9 copy-start.5
  46.7 2.2 %copy-start.8 = (bf16[64,64]{0,1:T(8,128)(2,1)S(1)}, bf16[64,64]{0,1:T(8,128)(2,1)}, u32[]{:S(2)}) copy-start(bf16[64,64]{0,1:T(8,128)(2,1)} %reshape.245) | copy-start | bytes 24580
  50.4 8.8 %copy-start.3 = (f32[128,2048]{1,0:T(8,128)S(1)}, f32[128,2048]{1,0:T(8,128)}, u32[]{:S(2)}) copy-start(f32[128,2048]{1,0:T(8,128)} %copy-done.2) | copy-start | bytes 3145732
  50.4 8.8 %slice-start.2 = ((f32[128,2048]{1,0:T(8,128)}), f32[128,1920]{1,0:T(8,128)S(1)}, s32[]{:S(2)}) async-start(f32[128,2048]{1,0:T(8,128)} %copy-done.2), calls=%async_computation.5 | async-start | bytes 1966080 | tf_op jit(solution)/shard_map/slice | solution.py:57
  53.0 34.1 %all-to-all-start.1 = ((bf16[8,16,4160]{2,1,0:T(8,128)(2,1)}), bf16[8,16,4160]{2,1,0:T(8,128)(2,1)}, u32[]{:S(2)}, u32[]{:S(2)}) async-start(bf16[8,16,4160]{2,1,0:T(8,128)(2,1)} %bitcast.86), calls=%async_computation.1 | async-start | bytes 2162688 | tf_op jit(solution)/shard_map/all_to_all | solution.py:171
  94.1 115.0 %all-to-all-start.2 = ((bf16[8,16,2048]{2,1,0:T(8,128)(2,1)}), bf16[8,16,2048]{2,1,0:T(8,128)(2,1)S(1)}, u32[]{:S(2)}, u32[]{:S(2)}) async-start(bf16[8,16,2048]{2,1,0:T(8,128)(2,1)} %bitcast.90), calls=%async_computation.2 | async-start | bytes 1048576 | tf_op jit(solution)/shard_map/all_to_all | solution.py:214
  97.8 11.2 %slice-start = ((s8[8388608]{0:T(1024)(128)(4,1)}), s8[4194304]{0:T(1024)(128)(4,1)S(1)}, s32[]{:S(2)}) async-start(s8[8388608]{0:T(1024)(128)(4,1)} %bitcast.82), calls=%async_computation.3 | async-start | bytes 8388608
  97.8 11.2 %slice-start.1 = ((s8[8388608]{0:T(1024)(128)(4,1)}), s8[4194304]{0:T(1024)(128)(4,1)S(1)}, s32[]{:S(2)}) async-start(s8[8388608]{0:T(1024)(128)(4,1)} %bitcast.82), calls=%async_computation.4 | async-start | bytes 8388608
  97.8 11.2 %copy-start.6 = (f32[128,2048]{1,0:T(8,128)S(1)}, f32[128,2048]{1,0:T(8,128)}, u32[]{:S(2)}) copy-start(f32[128,2048]{1,0:T(8,128)} %get-tuple-element.34) | copy-start | bytes 3145732
  97.8 11.2 %copy-start.7 = (f32[128,2048]{1,0:T(8,128)S(1)}, f32[128,2048]{1,0:T(8,128)}, u32[]{:S(2)}) copy-start(f32[128,2048]{1,0:T(8,128)} %get-tuple-element.36) | copy-start | bytes 3145732
  210.3 1.6 copy-start.4
